TPU v7x, 32 devices: a whole 2x2x4 slice. The times are simulated.
32 devices in a mesh: dp: 2 (over x), sp: 16 (over y, z, core).
Axes of the slice: x: 2, y: 2, z: 4, core: 2. Of those that a mesh axis runs over, the one named last changes fastest.
Arguments:
- q: bfloat16 [64, 32, 160], P('dp'), parts along dimension 0
- k: bfloat16 [64, 8192, 8, 160], P('dp', 'sp'), parts along dimension 0
- v: bfloat16 [64, 8192, 8, 160], P('dp', 'sp'), parts along dimension 0
Outputs:
- q: bfloat16 [64, 32, 160], P('dp'), parts along dimension 0
There are 2 independent parts. A program takes and returns all parts, laid end to end along the dimension named above; each array names one.
All inputs are finite; a program needn't handle non-finite values.
Results may differ from a plain program's by a relative error of at most 0.012.
Values are sent between devices in bfloat16 or wider.
A program may use at most 2 GiB of HBM per device.

v0:
```python
import jax
import jax.numpy as jnp
from jax import lax
from jax.sharding import PartitionSpec as P


def einsum(form, a, b):
    return jnp.einsum(form, a.astype(jnp.float32), b.astype(jnp.float32))


def part_of(q, k, v):
    grouped = q.reshape(q.shape[0], k.shape[2], -1, q.shape[2])
    scores = einsum("bgsd,bugd->bgsu", grouped, k) * q.shape[2] ** -0.5
    high = jnp.max(scores, -1, keepdims=True)
    weights = jnp.exp(scores - high)
    seen = einsum("bgsu,bugd->bgsd", weights.astype(jnp.bfloat16), v)
    return jnp.concatenate([seen, jnp.sum(weights, -1, keepdims=True), high], -1)


def together(parts):
    seen, total, high = parts[..., :-2], parts[..., -2:-1], parts[..., -1:]
    scale = jnp.exp(high - jnp.max(high, 0))
    return (jnp.sum(seen * scale, 0) / jnp.sum(total * scale, 0)).astype(jnp.bfloat16)


def solution(mesh):
    def step(q, k, v):
        return together(lax.all_gather(part_of(q, k, v), "sp")).reshape(q.shape)

    return jax.shard_map(
        step,
        mesh=mesh,
        in_specs=(P("dp", None, None), P("dp", "sp", None, None), P("dp", "sp", None, None)),
        out_specs=P("dp", None, None),
        check_vma=False,
    )
```

profile of v0, /device:TPU:0, one launch (start us, length us, event | category | flops | bytes accessed | tf_op | source)
XLA Modules:
  0.0 216.6 jit_solution(5820705413755366126)
XLA Ops:
  6.5 0.0 all-gather.3.cloned.1.call-start
  6.5 1.2 reshape.15
  7.7 15.8 %multiply_reduce_fusion = (f32[32,8,4]{2,1,0:T(8,128)S(1)}, f32[32,8,4,512]{3,2,1,0:T(4,128)S(1)}) fusion(bf16[32,8,4,160]{3,2,1,0:T(4,128)(2,1)S(1)} %reshape.15, bf16[32,512,8,160]{1,3,2,0:T(8,128)(2,1)} %param.4), kind=kOutput, calls=%fused_computation.3 | convolution fusion | flops 168819712 | bytes 44371968 | tf_op jit(solution)/shard_map/bgsd,bugd->bgsu/dot_general | solution.py:8
  23.6 1.2 fusion.1
  24.7 17.0 %fusion.3 = f32[32,8,4,160]{3,2,1,0:T(4,128)S(1)} fusion(bf16[32,512,8,160]{1,3,2,0:T(8,128)(2,1)} %param.5, f32[32,8,4,512]{3,2,1,0:T(4,128)S(1)} %get-tuple-element.11, f32[32,8,4]{2,1,0:T(8,128)S(1)} %get-tuple-element.10), kind=kOutput, calls=%fused_computation.6 | convolution fusion | flops 169345024 | bytes 44699648 | tf_op jit(solution)/shard_map/bgsu,bugd->bgsd/dot_general | solution.py:8
  41.7 1.7 copy.51
  43.4 1.7 copy.52
  45.0 0.7 pad_maximum_fusion
  45.7 1.2 copy.53
  46.9 0.0 all-gather.3.cloned.1.call-update
  46.9 128.6 %all-gather.3.cloned.1.call-done = f32[512,8,4,162]{3,1,2,0:T(8,128)} async-done(((f32[32,8,4,162]{3,1,2,0:T(8,128)}), f32[512,8,4,162]{3,1,2,0:T(8,128)}) %all-gather.3.cloned.1.call-update) | async-done | bytes 10616848 | tf_op jit(solution)/shard_map/all_gather | solution.py:28
  175.6 11.7 %fusion.10 = (f32[16,32,8,4,1]{4,2,3,1,0:T(8,128)}, f32[32,8,4]{1,2,0:T(4,128)S(1)}, f32[16,32,8,4,1]{4,2,3,1,0:T(8,128)}) fusion(f32[16,32,8,4,162]{4,2,3,1,0:T(8,128)} %bitcast.13), kind=kLoop, calls=%fused_computation.17 | loop fusion | flops 15360 | bytes 266240 | tf_op jit(solution)/shard_map/slice | solution.py:21
  187.3 6.3 %copy.65 = f32[16,32,8,4,1]{1,2,4,3,0:T(8,128)S(1)} copy(f32[16,32,8,4,1]{4,2,3,1,0:T(8,128)} %get-tuple-element.5) | data formatting | bytes 131072
  193.6 0.1 copy.66
  193.7 6.5 %copy.64 = f32[16,32,8,4,1]{1,2,4,3,0:T(8,128)S(1)} copy(f32[16,32,8,4,1]{4,2,3,1,0:T(8,128)} %get-tuple-element.7) | data formatting | bytes 131072
  200.2 0.1 multiply_reduce_fusion.1
  200.2 0.4 copy.55
  200.7 7.2 %fusion = f32[32,8,4,160]{3,1,2,0:T(8,128)S(1)} fusion(f32[16,32,8,4,162]{4,2,3,1,0:T(8,128)} %bitcast.14, f32[16,32,8,4]{2,3,1,0:T(4,128)S(1)} %copy.55), kind=kLoop, calls=%fused_computation.1 | loop fusion | flops 5079040 | bytes 11206656 | tf_op jit(solution)/shard_map/reduce_sum | solution.py:23
  207.9 0.6 copy.56
  208.5 0.2 fusion.5
  208.7 1.1 copy.59
  (1 shorter events, 0.0 us)
Async XLA Ops:
  6.5 169.0 %all-gather.3.cloned.1.call-start = ((), (), s32[]{:S(2)}) async-start(), calls=%async_computation | async-start | bytes 17825792 | tf_op jit(solution)/shard_map/all_gather | solution.py:28
Sparse Core Ops, SparseCore 0:
  47.1 128.4 all-gather.2
where the time goes:
time: 217 us
  waiting for transfers between devices  129 us (59%)
  matrix products  32.8 us (15%)
  other arithmetic  21 us (10%)
  local copies, waits for them, and re-layouts  20.7 us (10%)
  between operations  13.5 us (6%)
    all_gather x1, waiting for transfers between devices, step(): return together(lax.all_gather(part_of(q, k, v), 'sp')).reshape(q.shape)  129 us
    dot_general x2, matrix products, einsum(): return jnp.einsum(form, a.astype(jnp.float32), b.astype(jnp.float32))  32.8 us
    unnamed x3, local copies, waits for them, and re-layouts  12.9 us
    slice x1, other arithmetic, together(): seen, total, high = (parts[..., :-2], parts[..., -2:-1], parts[..., -1:])  11.7 us
    reduce_sum x1, other arithmetic, together(): jnp.sum(seen * scale, 0) / jnp.sum(total * scale, 0)  7.22 us
  transfers between devices with their start and end apart: 1, of which 1 were waited for; matrix products, arithmetic and copies ran while one was open for 0% of the time, Pallas kernels for 0%

commit v1 on v0

v1 whole, which is shorter than its diff:
```python
import functools
import jax
import jax.numpy as jnp
from jax import lax
from jax.experimental import pallas as pl
from jax.experimental.pallas import tpu as pltpu
from jax.sharding import PartitionSpec as P

MESH = pl.DeviceIdType.MESH
SLOTS = 8
LAG = 5
LOG2E = 1.4426950408889634


def owner_of(i):
    r = i % 16
    far, core, z, y = r // 8, r // 4 % 2, r // 2 % 2, r % 2
    return y * 8 + (far * (1 + z) + (1 - far) * 3 * z) * 2 + core


def kernel(
    q_hbm, k_hbm, v_hbm, out, q_ref, kbuf, vbuf, qbd, s_scr, part, stat, parts, stats,
    qsem, ksem, vsem, part_send, stat_send, part_recv, stat_recv, out_send, out_recv,
):
    n_seq, wide, tokens = k_hbm.shape
    heads, head = q_hbm.shape[1:]
    groups = wide // head
    per = heads // groups
    scale = head**-0.5
    me = lax.axis_index("sp")
    n_dev = parts.shape[1]

    def kcopy(i, slot):
        return pltpu.make_async_copy(k_hbm.at[i], kbuf.at[slot], ksem.at[slot])

    def vcopy(i, slot):
        return pltpu.make_async_copy(v_hbm.at[i], vbuf.at[slot], vsem.at[slot])

    qcopy = pltpu.make_async_copy(q_hbm, q_ref, qsem)
    qcopy.start()
    for i in range(SLOTS):
        kcopy(i, i).start()
        vcopy(i, i).start()

    barrier = pltpu.get_barrier_semaphore()
    for d in range(1, n_dev):
        pl.semaphore_signal(barrier, inc=1, device_id={"sp": (me + d) % n_dev}, device_id_type=MESH)

    col = lax.broadcasted_iota(jnp.int32, (head, wide), 1)
    row = lax.broadcasted_iota(jnp.int32, (head, wide), 0)
    spread = jnp.where(lax.rem(col, head) == row, 1.0, 0.0).astype(jnp.bfloat16)
    step = 4
    own = lax.broadcasted_iota(jnp.int32, (heads, wide), 0) // per == lax.broadcasted_iota(jnp.int32, (heads, wide), 1) // head
    qcopy.wait()

    def spread_one(b, _):
        x = q_ref[pl.ds(b * step, step)].reshape(step * heads, head)
        y = jnp.dot(x, spread, preferred_element_type=jnp.float32)
        for s in range(step):
            qbd[b * step + s] = jnp.where(own, y[s * heads : (s + 1) * heads], 0.0).astype(jnp.bfloat16)
        return 0

    lax.fori_loop(0, n_seq // step, spread_one, 0)

    sub = lax.broadcasted_iota(jnp.int32, (8, head), 0) < per
    lane = lax.broadcasted_iota(jnp.int32, (heads, 128), 1)

    def scores(i, slot):
        return jnp.dot(qbd[i], kbuf[slot], preferred_element_type=jnp.float32)

    def values(i, slot, s):
        high = jnp.max(s, -1, keepdims=True)
        p = jnp.exp2((s - high) * (scale * LOG2E))
        total = jnp.sum(p, -1, keepdims=True)
        pb = p.astype(jnp.bfloat16)
        outs = []
        for j in range(heads // 16):
            half = pb[16 * j : 16 * j + 16]
            o = [
                lax.dot_general(half, vbuf[slot, pl.ds((4 * j + g) * head, head)], (((1,), (1,)), ((), ())), preferred_element_type=jnp.float32)
                for g in range(4)
            ]
            for t in range(2):
                outs.append(jnp.where(sub, o[2 * t][8 * t : 8 * t + 8], o[2 * t + 1][8 * t : 8 * t + 8]))
        part[i] = jnp.concatenate(outs, 0).astype(jnp.bfloat16)
        stat[i] = jnp.where(lane == 0, high * scale, total).T[:2, :heads]

    def part_copies(i, rd, to):
        return (
            pltpu.make_async_remote_copy(part.at[i], parts.at[rd, me], part_send, part_recv.at[rd], device_id={"sp": to}, device_id_type=MESH),
            pltpu.make_async_remote_copy(stat.at[i], stats.at[rd, me], stat_send, stat_recv.at[rd], device_id={"sp": to}, device_id_type=MESH),
        )

    def send(i, rd, to):
        @pl.when(to != me)
        def _():
            for copy in part_copies(i, rd, to):
                copy.start()

        @pl.when(to == me)
        def _():
            parts[rd, me] = part[i]
            stats[rd, me] = stat[i]

    def together(i, rd, to):
        @pl.when(to == me)
        def _():
            others = pl.ds(0, n_dev - 1)
            for ref, recv in ((parts, part_recv), (stats, stat_recv)):
                pltpu.make_async_remote_copy(ref.at[rd, others], ref.at[rd, others], part_send, recv.at[rd], device_id={"sp": me}, device_id_type=MESH).wait_recv()
            highs = [stats[rd, d, 0:1] for d in range(n_dev)]
            totals = [stats[rd, d, 1:2] for d in range(n_dev)]
            high = functools.reduce(jnp.maximum, highs)
            shares = [jnp.exp(h - high) for h in highs]
            total = functools.reduce(jnp.add, [a * b for a, b in zip(shares, totals)])
            shares = jnp.concatenate(shares, 0) / total
            shares = shares.T
            acc = None
            for d in range(n_dev):
                term = parts[rd, d].astype(jnp.float32) * shares[:, d : d + 1]
                acc = term if acc is None else acc + term
            out[i] = acc.astype(jnp.bfloat16)
            for d in range(1, n_dev):
                pltpu.make_async_remote_copy(out.at[i], out.at[i], out_send, out_recv, device_id={"sp": (me + d) % n_dev}, device_id_type=MESH).start()

    kcopy(0, 0).wait()
    s_scr[...] = scores(0, 0)
    kcopy(SLOTS, 0).start()
    pl.semaphore_wait(barrier, n_dev - 1)

    def trip(c, last):
        for j in range(SLOTS):
            i = c * SLOTS + j
            after = (j + 1) % SLOTS
            more = not (last and j == SLOTS - 1)
            if more:
                kcopy(i + 1, after).wait()
            vcopy(i, j).wait()
            s = s_scr[...]
            values(i, j, s)
            if more:
                s_scr[...] = scores(i + 1, after)
            if not last:
                vcopy(i + SLOTS, j).start()
                if j < SLOTS - 1:
                    kcopy(i + 1 + SLOTS, after).start()
                else:

                    @pl.when(c < n_seq // SLOTS - 2)
                    def _():
                        kcopy(i + 1 + SLOTS, after).start()

            def sent(e=i - 1):
                send(e, e // 16, owner_of(e))

            if j > 0 or last:
                sent()
            else:
                pl.when(c > 0)(sent)

            def joined(e=i - LAG):
                together(e, e // 16, owner_of(e))

            if j >= LAG or last:
                joined()
            else:
                pl.when(c > 0)(joined)

    def body(c, _):
        trip(c, False)
        return 0

    trips = n_seq // SLOTS
    lax.fori_loop(0, trips - 1, body, 0)
    trip(trips - 1, True)
    send(n_seq - 1, 1, owner_of(n_seq - 1))
    for e in range(n_seq - LAG, n_seq):
        together(e, 1, owner_of(e))

    count = pl.ds(0, n_seq - 2)
    everyone = {"device_id": {"sp": me}, "device_id_type": MESH}
    pltpu.make_async_remote_copy(part.at[count], part.at[count], part_send, out_recv, **everyone).wait_send()
    pltpu.make_async_remote_copy(stat.at[count], stat.at[count], stat_send, out_recv, **everyone).wait_send()
    finished = pltpu.make_async_remote_copy(out.at[count], out.at[count], out_send, out_recv, **everyone)
    finished.wait_send()
    finished.wait_recv()


def attend(q, k, v, n_dev):
    n, heads, head = q.shape
    tokens, groups = k.shape[1:3]
    wide = groups * head
    kt = k.transpose(0, 2, 3, 1).reshape(n, wide, tokens)
    vt = v.transpose(0, 2, 3, 1).reshape(n, wide, tokens)
    dma = pltpu.SemaphoreType.DMA
    return pl.pallas_call(
        kernel,
        out_shape=jax.ShapeDtypeStruct((n, heads, head), jnp.bfloat16),
        in_specs=[pl.BlockSpec(memory_space=pl.ANY)] * 3,
        out_specs=pl.BlockSpec(memory_space=pltpu.VMEM),
        scratch_shapes=[
            pltpu.VMEM((n, heads, head), jnp.bfloat16),
            pltpu.VMEM((SLOTS, wide, tokens), jnp.bfloat16),
            pltpu.VMEM((SLOTS, wide, tokens), jnp.bfloat16),
            pltpu.VMEM((n, heads, wide), jnp.bfloat16),
            pltpu.VMEM((heads, tokens), jnp.float32),
            pltpu.VMEM((n, heads, head), jnp.bfloat16),
            pltpu.VMEM((n, 2, heads), jnp.float32),
            pltpu.VMEM((2, n_dev, heads, head), jnp.bfloat16),
            pltpu.VMEM((2, n_dev, 2, heads), jnp.float32),
            dma(()), dma((SLOTS,)), dma((SLOTS,)), dma(()), dma(()), dma((2,)), dma((2,)), dma(()), dma(()),
        ],
        compiler_params=pltpu.CompilerParams(vmem_limit_bytes=60 * 1024 * 1024, collective_id=0, has_side_effects=True),
    )(q, kt, vt)


def solution(mesh):
    n_dev = mesh.shape["sp"]

    return jax.shard_map(
        lambda q, k, v: attend(q, k, v, n_dev),
        mesh=mesh,
        in_specs=(P("dp", None, None), P("dp", "sp", None, None), P("dp", "sp", None, None)),
        out_specs=P("dp", None, None),
        check_vma=False,
    )
```

time: 217 us -> 56.1 us (0.26)
  waiting for transfers between devices: 129 us -> 0 us
  Pallas kernels: 0 us -> 54 us
  matrix products: 32.8 us -> 0 us
  other arithmetic: 21 us -> 0 us
  local copies, waits for them, and re-layouts: 20.7 us -> 1.87 us
  between operations: 13.5 us -> 0.01 us
    all_gather x1 -> x0, waiting for transfers between devices: 129 us -> none  [step(): return together(lax.all_gather(part_of(q, k, v), 'sp')).reshape(q.shape)]
    pallas_call x0 -> x1, Pallas kernels: none -> 54 us  [attend(): pl.pallas_call(kernel, out_shape=jax.ShapeDtypeStruct((n, heads, head), j...]
    dot_general x2 -> x0, matrix products: 32.8 us -> none  [einsum(): return jnp.einsum(form, a.astype(jnp.float32), b.astype(jnp.float32))]
    slice x1 -> x0, other arithmetic: 11.7 us -> none  [together(): seen, total, high = (parts[..., :-2], parts[..., -2:-1], parts[..., -1:])]
    unnamed x3 -> x1, local copies, waits for them, and re-layouts: 12.9 us -> 1.87 us
    reduce_sum x3 -> x0, other arithmetic: 8.44 us -> none  [the longest x1 7.22 us: together(): jnp.sum(seen * scale, 0) / jnp.sum(total * scale, 0)]
    broadcast_in_dim x2 -> x0, local copies, waits for them, and re-layouts: 3.33 us -> none  [the longest x1 1.66 us: part_of(): jnp.sum(weights, -1, keepdims=True)]
  transfers between devices with their start and end apart: 1 -> 0, of which waited for: 1 -> 0; matrix products, arithmetic and copies ran while one was open for 0% -> 0% of each run, Pallas kernels for 0% -> 0%
where the time goes in v1:
time: 56.1 us; the launch traced here: 55.9 us
  Pallas kernels  54 us (96%)
  local copies, waits for them, and re-layouts  1.87 us (3%)
    pallas_call x1, Pallas kernels, attend(): pl.pallas_call(kernel, out_shape=jax.ShapeDtypeStruct((n, heads, head), j...  54 us
    unnamed x1, local copies, waits for them, and re-layouts  1.87 us

profile of v1, /device:TPU:0, one launch (start us, length us, event | category | flops | bytes accessed | tf_op | source)
XLA Modules:
  0.0 55.9 jit_solution(7999852959657504250)
XLA Ops:
  0.0 54.0 %shard_map.37 = bf16[32,32,160]{2,1,0:T(8,128)(2,1)} custom-call(bf16[32,32,160]{2,1,0:T(8,128)(2,1)} %q_hbm.1, bf16[32,1280,512]{2,1,0:T(8,128)(2,1)} %bitcast.6, bf16[32,1280,512]{2,1,0:T(8,128)(2,1)} %bitcast.7), custom_call_target="tpu_custom_call" | custom-call | tf_op jit(solution)/shard_map/pallas_call | solution.py:196
  54.0 1.9 %copy.5 = bf16[32,32,160]{2,1,0:T(8,128)(2,1)} copy(bf16[32,32,160]{2,1,0:T(8,128)(2,1)} %shard_map.37) | data formatting | bytes 655360

commit v2 on v0

v2 whole, which is shorter than its diff:
```python
import functools
import jax
import jax.numpy as jnp
from jax import lax
from jax.experimental import pallas as pl
from jax.experimental.pallas import tpu as pltpu
from jax.sharding import PartitionSpec as P

MESH = pl.DeviceIdType.MESH
KAHEAD, VAHEAD = 3, 3
SLOTS = 8
PAIR, OWNER, HAND = 3, 12, 20
LOG2E = 1.4426950408889634


def chip_of(i):
    h = i // 2 % 8
    far, z, y = h // 4, h // 2 % 2, h % 2
    return y * 4 + far * (1 + z) + (1 - far) * 3 * z


def kernel(
    q_hbm, k_hbm, v_hbm, out, q_ref, kbuf, vbuf, s_scr, mine, theirs, part, stat, parts, stats,
    qsem, ksem, vsem, pair_send, pair_recv, part_send, stat_send, part_recv, stat_recv, out_send, out_recv, hand_send, hand_recv,
):
    n_seq, wide, tokens = k_hbm.shape
    heads, head = q_hbm.shape[1:]
    groups = wide // head
    per = heads // groups
    scale = head**-0.5
    me = lax.axis_index("sp")
    chip, core = me // 2, me % 2
    other = chip * 2 + 1 - core
    chips = parts.shape[1]
    tail = head - 128

    def remote(src, dst, send, recv, to):
        return pltpu.make_async_remote_copy(src, dst, send, recv, device_id={"sp": to}, device_id_type=MESH)

    def kcopy(i, slot):
        return pltpu.make_async_copy(k_hbm.at[i], kbuf.at[slot], ksem.at[slot])

    def vcopy(i, slot):
        return pltpu.make_async_copy(v_hbm.at[i], vbuf.at[slot], vsem.at[slot])

    qcopy = pltpu.make_async_copy(q_hbm, q_ref, qsem)
    qcopy.start()
    for i in range(KAHEAD + 1):
        kcopy(i, i).start()
        if i < VAHEAD:
            vcopy(i, i).start()

    barrier = pltpu.get_barrier_semaphore()
    for d in range(1, chips):
        pl.semaphore_signal(barrier, inc=1, device_id={"sp": (me + 2 * d) % (2 * chips)}, device_id_type=MESH)
    pl.semaphore_signal(barrier, inc=1, device_id={"sp": other}, device_id_type=MESH)

    row = lax.broadcasted_iota(jnp.int32, (16, tokens), 0) // per
    lane = lax.broadcasted_iota(jnp.int32, (heads, 128), 1)
    lane8 = lax.broadcasted_iota(jnp.int32, (8, 128), 1) // tail

    def only(x, g):
        return jnp.where(row[:, : x.shape[1]] == g, x, jnp.zeros_like(x))

    def scores(i, slot):
        halves = []
        for j in range(heads // 16):
            q = q_ref[i, 16 * j : 16 * j + 16]
            halves.append(
                sum(
                    jnp.dot(only(q, g), kbuf[slot, pl.ds((4 * j + g) * head, head)], preferred_element_type=jnp.float32)
                    for g in range(16 // per)
                )
            )
        return jnp.concatenate(halves, 0)

    def values(i, slot, s):
        high = jnp.max(s, -1, keepdims=True)
        p = jnp.exp2((s - high) * (scale * LOG2E))
        total = jnp.sum(p, -1, keepdims=True)
        pb = p.astype(jnp.bfloat16)
        mine[i, 1] = jnp.where(lane == 64, high * scale, total)
        for j in range(heads // 16):
            half = pb[16 * j : 16 * j + 16]
            o = sum(
                lax.dot_general(only(half, g), vbuf[slot, pl.ds((4 * j + g) * head, head)], (((1,), (1,)), ((), ())), preferred_element_type=jnp.float32)
                for g in range(16 // per)
            )
            mine[i, 0, 16 * j : 16 * j + 16] = o[:, :128]
            mine[i, 1, 16 * j : 16 * j + 16, :tail] = o[:, 128:]

    def pair_copy(i):
        return remote(mine.at[i], theirs.at[i // 2], pair_send, pair_recv.at[i // 2], other)

    def give(i):
        @pl.when(core != i % 2)
        def _():
            pair_copy(i).start()

    def pair(i):
        @pl.when(core == i % 2)
        def _():
            h, rd, to = i // 2, i // 16, chip_of(i)
            pair_copy(i).wait_recv()
            a0, a1, b0, b1 = mine[i, 0], mine[i, 1], theirs[h, 0], theirs[h, 1]
            ah, at, bh, bt = a1[:, 64:65], a1[:, 65:66], b1[:, 64:65], b1[:, 65:66]
            high = jnp.maximum(ah, bh)
            fa, fb = jnp.exp(ah - high), jnp.exp(bh - high)
            total = at * fa + bt * fb
            o0 = a0 * fa + b0 * fb
            o1 = a1 * fa + b1 * fb
            packed = o1[0:8]
            for j in range(1, heads // 8):
                packed = jnp.where(lane8 == j, pltpu.roll(o1[8 * j : 8 * j + 8], tail * j, 1), packed)
            part[h] = jnp.concatenate([o0, packed], 0).astype(jnp.bfloat16)
            stat[h] = jnp.where(lane == 0, high, total).T[:2, :heads]

            @pl.when(to != chip)
            def _():
                remote(part.at[h], parts.at[rd, chip], part_send, part_recv.at[rd], 2 * to + core).start()
                remote(stat.at[h], stats.at[rd, chip], stat_send, stat_recv.at[rd], 2 * to + core).start()

            @pl.when(to == chip)
            def _():
                parts[rd, chip] = part[h]
                stats[rd, chip] = stat[h]

    def together(i):
        rd = i // 16

        @pl.when(2 * chip_of(i) + i % 2 == me)
        def _():
            others = pl.ds(0, chips - 1)
            remote(parts.at[rd, others], parts.at[rd, others], part_send, part_recv.at[rd], other).wait_recv()
            remote(stats.at[rd, others], stats.at[rd, others], stat_send, stat_recv.at[rd], other).wait_recv()
            highs = [stats[rd, d, 0:1] for d in range(chips)]
            totals = [stats[rd, d, 1:2] for d in range(chips)]
            high = functools.reduce(jnp.maximum, highs)
            shares = [jnp.exp(h - high) for h in highs]
            total = functools.reduce(jnp.add, [a * b for a, b in zip(shares, totals)])
            shares = (jnp.concatenate(shares, 0) / total).T
            acc0 = acc1 = None
            for d in range(chips):
                share = jnp.broadcast_to(shares[:, d : d + 1], (heads, 128))
                packed = share[0:8]
                for j in range(1, heads // 8):
                    packed = jnp.where(lane8 == j, share[8 * j : 8 * j + 8], packed)
                x = parts[rd, d].astype(jnp.float32)
                t0, t1 = x[:heads] * share, x[heads:] * packed
                acc0, acc1 = (t0, t1) if d == 0 else (acc0 + t0, acc1 + t1)
            out[i, :, :128] = acc0.astype(jnp.bfloat16)
            rest = [acc1] + [pltpu.roll(acc1, 128 - tail * j, 1) for j in range(1, heads // 8)]
            out[i, :, 128:] = jnp.concatenate(rest, 0)[:, :tail].astype(jnp.bfloat16)
            for d in range(1, chips):
                remote(out.at[i], out.at[i], out_send, out_recv.at[i // 2], (me + 2 * d) % (2 * chips)).start()
            remote(out.at[i], out.at[i], hand_send, hand_recv, other).start()

    def hand(i):
        @pl.when((core == i % 2) & (chip_of(i) != chip))
        def _():
            remote(out.at[i], out.at[i], out_send, out_recv.at[i // 2], other).wait_recv()
            remote(out.at[i], out.at[i], hand_send, hand_recv, other).start()

    qcopy.wait()
    kcopy(0, 0).wait()
    s_scr[...] = scores(0, 0)

    def trip(c, last):
        for j in range(SLOTS):
            i = c * SLOTS + j
            after = (j + 1) % SLOTS
            more = not (last and j == SLOTS - 1)
            if not last or j + VAHEAD < SLOTS:
                vcopy(i + VAHEAD, (j + VAHEAD) % SLOTS).start()
            if not last or j + 1 + KAHEAD < SLOTS:
                kcopy(i + 1 + KAHEAD, (j + 1 + KAHEAD) % SLOTS).start()
            if more:
                kcopy(i + 1, after).wait()
            vcopy(i, j).wait()
            s = s_scr[...]
            if more:
                later = scores(i + 1, after)
            values(i, j, s)
            if more:
                s_scr[...] = later

            def at(lag, f, e):
                if last or j >= lag:
                    f(e)
                elif lag - j <= (n_seq // SLOTS - 2) * SLOTS:
                    pl.when(c >= -((j - lag) // SLOTS))(lambda: f(e))

            if j == 0:
                if not last:
                    pl.when(c == 0)(lambda: pl.semaphore_wait(barrier, chips))
            at(1, give, i - 1)
            at(PAIR, pair, i - PAIR)
            at(OWNER, together, i - OWNER)
            at(HAND, hand, i - HAND)

    def body(c, _):
        trip(c, False)
        return 0

    trips = n_seq // SLOTS
    lax.fori_loop(0, trips - 1, body, 0)
    trip(trips - 1, True)
    give(n_seq - 1)
    for i in range(n_seq - PAIR, n_seq):
        pair(i)
    late = [(i + OWNER, together, i) for i in range(n_seq - OWNER, n_seq)] + [(i + HAND, hand, i) for i in range(n_seq - HAND, n_seq)]
    for _, f, i in sorted(late, key=lambda x: x[0]):
        f(i)

    half = pl.ds(0, n_seq // 2)
    remote(mine.at[half], mine.at[half], pair_send, hand_recv, other).wait_send()
    sent = pl.ds(0, n_seq // 2 - 2)
    remote(part.at[sent], part.at[sent], part_send, hand_recv, other).wait_send()
    remote(stat.at[sent], stat.at[sent], stat_send, hand_recv, other).wait_send()
    sent = pl.ds(0, 2 * (chips - 1))
    remote(out.at[sent], out.at[sent], out_send, hand_recv, other).wait_send()
    handed = remote(out.at[half], out.at[half], hand_send, hand_recv, other)
    handed.wait_send()
    handed.wait_recv()


def attend(q, k, v, n_dev):
    n, heads, head = q.shape
    tokens, groups = k.shape[1:3]
    wide, chips = groups * head, n_dev // 2
    kt = k.transpose(0, 2, 3, 1).reshape(n, wide, tokens)
    vt = v.transpose(0, 2, 3, 1).reshape(n, wide, tokens)
    dma = pltpu.SemaphoreType.DMA
    packed = heads + heads * (head - 128) // 128
    return pl.pallas_call(
        kernel,
        out_shape=pltpu.VMEM((n, heads, head), jnp.bfloat16),
        in_specs=[pl.BlockSpec(memory_space=pltpu.HBM)] * 3,
        out_specs=pl.BlockSpec(memory_space=pltpu.VMEM),
        scratch_shapes=[
            pltpu.VMEM((n, heads, head), jnp.bfloat16),
            pltpu.VMEM((SLOTS, wide, tokens), jnp.bfloat16),
            pltpu.VMEM((SLOTS, wide, tokens), jnp.bfloat16),
            pltpu.VMEM((heads, tokens), jnp.float32),
            pltpu.VMEM((n, 2, heads, 128), jnp.float32),
            pltpu.VMEM((n // 2, 2, heads, 128), jnp.float32),
            pltpu.VMEM((n // 2, packed, 128), jnp.bfloat16),
            pltpu.VMEM((n // 2, 2, heads), jnp.float32),
            pltpu.VMEM((2, chips, packed, 128), jnp.bfloat16),
            pltpu.VMEM((2, chips, 2, heads), jnp.float32),
            dma(()), dma((SLOTS,)), dma((SLOTS,)), dma(()), dma((n // 2,)), dma(()), dma(()), dma((2,)), dma((2,)),
            dma(()), dma((n // 2,)), dma(()), dma(()),
        ],
        compiler_params=pltpu.CompilerParams(vmem_limit_bytes=60 * 1024 * 1024, collective_id=0, has_side_effects=True),
    )(q, kt, vt)


def solution(mesh):
    n_dev = mesh.shape["sp"]

    return jax.shard_map(
        lambda q, k, v: attend(q, k, v, n_dev),
        mesh=mesh,
        in_specs=(P("dp", None, None), P("dp", "sp", None, None), P("dp", "sp", None, None)),
        out_specs=P("dp", None, None),
        check_vma=False,
    )
```

time: 217 us -> 41.7 us (0.19)
  waiting for transfers between devices: 129 us -> 0 us
  Pallas kernels: 0 us -> 40.8 us
  matrix products: 32.8 us -> 0 us
  other arithmetic: 21 us -> 0 us
  local copies, waits for them, and re-layouts: 20.7 us -> 0.8 us
  between operations: 13.5 us -> 0.01 us
    all_gather x1 -> x0, waiting for transfers between devices: 129 us -> none  [step(): return together(lax.all_gather(part_of(q, k, v), 'sp')).reshape(q.shape)]
    pallas_call x0 -> x1, Pallas kernels: none -> 40.8 us  [attend(): pl.pallas_call(kernel, out_shape=pltpu.VMEM((n, heads, head), jnp.bfloat1...]
    dot_general x2 -> x0, matrix products: 32.8 us -> none  [einsum(): return jnp.einsum(form, a.astype(jnp.float32), b.astype(jnp.float32))]
    unnamed x3 -> x1, local copies, waits for them, and re-layouts: 12.9 us -> 0.8 us
    slice x1 -> x0, other arithmetic: 11.7 us -> none  [together(): seen, total, high = (parts[..., :-2], parts[..., -2:-1], parts[..., -1:])]
    reduce_sum x3 -> x0, other arithmetic: 8.44 us -> none  [the longest x1 7.22 us: together(): jnp.sum(seen * scale, 0) / jnp.sum(total * scale, 0)]
    broadcast_in_dim x2 -> x0, local copies, waits for them, and re-layouts: 3.33 us -> none  [the longest x1 1.66 us: part_of(): jnp.sum(weights, -1, keepdims=True)]
  transfers between devices with their start and end apart: 1 -> 0, of which waited for: 1 -> 0; matrix products, arithmetic and copies ran while one was open for 0% -> 0% of each run, Pallas kernels for 0% -> 0%
where the time goes in v2:
time: 41.7 us; the launch traced here: 41.6 us
  Pallas kernels  40.8 us (98%)
  local copies, waits for them, and re-layouts  0.8 us (2%)
    pallas_call x1, Pallas kernels, attend(): pl.pallas_call(kernel, out_shape=pltpu.VMEM((n, heads, head), jnp.bfloat1...  40.8 us

profile of v2, /device:TPU:0, one launch (start us, length us, event | category | flops | bytes accessed | tf_op | source)
XLA Modules:
  0.0 41.6 jit_solution(15054228467072093659)
XLA Ops:
  0.0 40.8 %shard_map.37 = bf16[32,32,160]{2,1,0:T(8,128)(2,1)S(1)} custom-call(bf16[32,32,160]{2,1,0:T(8,128)(2,1)} %q_hbm.1, bf16[32,1280,512]{2,1,0:T(8,128)(2,1)} %bitcast.6, bf16[32,1280,512]{2,1,0:T(8,128)(2,1)} %bitcast.7), custom_call_target="tpu_custom_call" | custom-call | tf_op jit(solution)/shard_map/pallas_call | solution.py:235
  40.8 0.8 %copy.5 = bf16[32,32,160]{2,1,0:T(8,128)(2,1)} copy(bf16[32,32,160]{2,1,0:T(8,128)(2,1)S(1)} %shard_map.37) | data formatting | bytes 655360

commit v3 on v2

--- a/solution.py
+++ b/solution.py
@@ -7,7 +7,9 @@
 from jax.sharding import PartitionSpec as P
 
 MESH = pl.DeviceIdType.MESH
-KAHEAD, VAHEAD = 3, 3
+AHEAD, LESS = 3, 3
+LATE = 2
+LAST = 4
 SLOTS = 8
 PAIR, OWNER, HAND = 3, 12, 20
 LOG2E = 1.4426950408889634
@@ -20,8 +22,8 @@
 
 
 def kernel(
-    q_hbm, k_hbm, v_hbm, out, q_ref, kbuf, vbuf, s_scr, mine, theirs, part, stat, parts, stats,
-    qsem, ksem, vsem, pair_send, pair_recv, part_send, stat_send, part_recv, stat_recv, out_send, out_recv, hand_send, hand_recv,
+    q_hbm, k_hbm, v_hbm, out, q_ref, kbuf, vbuf, s_scr, mine, theirs, part, stat, parts, stats, all_parts, all_stats,
+    qsem, ksem, vsem, pair_send, pair_recv, part_send, stat_send, part_recv, stat_recv, out_send, out_recv, hand_send, hand_recv, all_send, all_recv,
 ):
     n_seq, wide, tokens = k_hbm.shape
     heads, head = q_hbm.shape[1:]
@@ -33,6 +35,7 @@
     other = chip * 2 + 1 - core
     chips = parts.shape[1]
     tail = head - 128
+    owned = n_seq - LAST
 
     def remote(src, dst, send, recv, to):
         return pltpu.make_async_remote_copy(src, dst, send, recv, device_id={"sp": to}, device_id_type=MESH)
@@ -43,12 +46,16 @@
     def vcopy(i, slot):
         return pltpu.make_async_copy(v_hbm.at[i], vbuf.at[slot], vsem.at[slot])
 
-    qcopy = pltpu.make_async_copy(q_hbm, q_ref, qsem)
-    qcopy.start()
-    for i in range(KAHEAD + 1):
+    first, rest = (
+        pltpu.make_async_copy(q_hbm.at[part_of_q], q_ref.at[part_of_q], qsem.at[x])
+        for x, part_of_q in enumerate((pl.ds(0, SLOTS), pl.ds(SLOTS, n_seq - SLOTS)))
+    )
+    first.start()
+    for i in range(AHEAD):
         kcopy(i, i).start()
-        if i < VAHEAD:
-            vcopy(i, i).start()
+        vcopy(i, i).start()
+    rest.start()
+    kcopy(AHEAD, AHEAD).start()
 
     barrier = pltpu.get_barrier_semaphore()
     for d in range(1, chips):
@@ -113,6 +120,19 @@
             for j in range(1, heads // 8):
                 packed = jnp.where(lane8 == j, pltpu.roll(o1[8 * j : 8 * j + 8], tail * j, 1), packed)
             part[h] = jnp.concatenate([o0, packed], 0).astype(jnp.bfloat16)
+
+            if isinstance(i, int) and i >= owned:
+                slot = h - (n_seq - LAST) // 2
+                peers = [(me + 2 * d) % (2 * chips) for d in range(1, chips)]
+                for peer in peers:
+                    remote(part.at[h], all_parts.at[slot, chip], all_send.at[0], all_recv.at[slot, 0], peer).start()
+                stat[h] = jnp.where(lane == 0, high, total).T[:2, :heads]
+                for peer in peers:
+                    remote(stat.at[h], all_stats.at[slot, chip], all_send.at[1], all_recv.at[slot, 1], peer).start()
+                all_parts[slot, chip] = part[h]
+                all_stats[slot, chip] = stat[h]
+                return
+
             stat[h] = jnp.where(lane == 0, high, total).T[:2, :heads]
 
             @pl.when(to != chip)
@@ -125,35 +145,45 @@
                 parts[rd, chip] = part[h]
                 stats[rd, chip] = stat[h]
 
+    def result(i, parts, stats, recv_part, recv_stat):
+        others = pl.ds(0, chips - 1)
+        remote(parts.at[others], parts.at[others], part_send, recv_part, other).wait_recv()
+        remote(stats.at[others], stats.at[others], stat_send, recv_stat, other).wait_recv()
+        highs = [stats[d, 0:1] for d in range(chips)]
+        totals = [stats[d, 1:2] for d in range(chips)]
+        high = functools.reduce(jnp.maximum, highs)
+        shares = [jnp.exp(h - high) for h in highs]
+        total = functools.reduce(jnp.add, [a * b for a, b in zip(shares, totals)])
+        shares = (jnp.concatenate(shares, 0) / total).T
+        acc0 = acc1 = None
+        for d in range(chips):
+            share = jnp.broadcast_to(shares[:, d : d + 1], (heads, 128))
+            packed = share[0:8]
+            for j in range(1, heads // 8):
+                packed = jnp.where(lane8 == j, share[8 * j : 8 * j + 8], packed)
+            x = parts[d].astype(jnp.float32)
+            t0, t1 = x[:heads] * share, x[heads:] * packed
+            acc0, acc1 = (t0, t1) if d == 0 else (acc0 + t0, acc1 + t1)
+        out[i, :, :128] = acc0.astype(jnp.bfloat16)
+        rest = [acc1] + [pltpu.roll(acc1, 128 - tail * j, 1) for j in range(1, heads // 8)]
+        out[i, :, 128:] = jnp.concatenate(rest, 0)[:, :tail].astype(jnp.bfloat16)
+        remote(out.at[i], out.at[i], hand_send, hand_recv, other).start()
+
     def together(i):
         rd = i // 16
 
         @pl.when(2 * chip_of(i) + i % 2 == me)
         def _():
-            others = pl.ds(0, chips - 1)
-            remote(parts.at[rd, others], parts.at[rd, others], part_send, part_recv.at[rd], other).wait_recv()
-            remote(stats.at[rd, others], stats.at[rd, others], stat_send, stat_recv.at[rd], other).wait_recv()
-            highs = [stats[rd, d, 0:1] for d in range(chips)]
-            totals = [stats[rd, d, 1:2] for d in range(chips)]
-            high = functools.reduce(jnp.maximum, highs)
-            shares = [jnp.exp(h - high) for h in highs]
-            total = functools.reduce(jnp.add, [a * b for a, b in zip(shares, totals)])
-            shares = (jnp.concatenate(shares, 0) / total).T
-            acc0 = acc1 = None
-            for d in range(chips):
-                share = jnp.broadcast_to(shares[:, d : d + 1], (heads, 128))
-                packed = share[0:8]
-                for j in range(1, heads // 8):
-                    packed = jnp.where(lane8 == j, share[8 * j : 8 * j + 8], packed)
-                x = parts[rd, d].astype(jnp.float32)
-                t0, t1 = x[:heads] * share, x[heads:] * packed
-                acc0, acc1 = (t0, t1) if d == 0 else (acc0 + t0, acc1 + t1)
-            out[i, :, :128] = acc0.astype(jnp.bfloat16)
-            rest = [acc1] + [pltpu.roll(acc1, 128 - tail * j, 1) for j in range(1, heads // 8)]
-            out[i, :, 128:] = jnp.concatenate(rest, 0)[:, :tail].astype(jnp.bfloat16)
+            result(i, parts.at[rd], stats.at[rd], part_recv.at[rd], stat_recv.at[rd])
             for d in range(1, chips):
                 remote(out.at[i], out.at[i], out_send, out_recv.at[i // 2], (me + 2 * d) % (2 * chips)).start()
-            remote(out.at[i], out.at[i], hand_send, hand_recv, other).start()
+
+    def everywhere(i):
+        slot = i // 2 - (n_seq - LAST) // 2
+
+        @pl.when(core == i % 2)
+        def _():
+            result(i, all_parts.at[slot], all_stats.at[slot], all_recv.at[slot, 0], all_recv.at[slot, 1])
 
     def hand(i):
         @pl.when((core == i % 2) & (chip_of(i) != chip))
@@ -161,19 +191,28 @@
             remote(out.at[i], out.at[i], out_send, out_recv.at[i // 2], other).wait_recv()
             remote(out.at[i], out.at[i], hand_send, hand_recv, other).start()
 
-    qcopy.wait()
+    first.wait()
     kcopy(0, 0).wait()
     s_scr[...] = scores(0, 0)
+
+    start = n_seq - SLOTS
+    done = [start - 1, start - PAIR, start - OWNER, start - HAND]
+
+    def lags(j):
+        return 0, LATE, OWNER - min(j // 2, 2), HAND - min(j // 2, 2)
 
     def trip(c, last):
         for j in range(SLOTS):
             i = c * SLOTS + j
             after = (j + 1) % SLOTS
             more = not (last and j == SLOTS - 1)
-            if not last or j + VAHEAD < SLOTS:
-                vcopy(i + VAHEAD, (j + VAHEAD) % SLOTS).start()
-            if not last or j + 1 + KAHEAD < SLOTS:
-                kcopy(i + 1 + KAHEAD, (j + 1 + KAHEAD) % SLOTS).start()
+            ahead = LESS if last else AHEAD
+            if not last or AHEAD <= j + ahead < SLOTS:
+                vcopy(i + ahead, (j + ahead) % SLOTS).start()
+            if not last or AHEAD < j + 1 + ahead < SLOTS:
+                kcopy(i + 1 + ahead, (j + 1 + ahead) % SLOTS).start()
+            if not last and j == SLOTS - 2:
+                pl.when(c == 0)(rest.wait)
             if more:
                 kcopy(i + 1, after).wait()
             vcopy(i, j).wait()
@@ -193,10 +232,16 @@
             if j == 0:
                 if not last:
                     pl.when(c == 0)(lambda: pl.semaphore_wait(barrier, chips))
-            at(1, give, i - 1)
-            at(PAIR, pair, i - PAIR)
-            at(OWNER, together, i - OWNER)
-            at(HAND, hand, i - HAND)
+            if not last:
+                at(1, give, i - 1)
+                at(PAIR, pair, i - PAIR)
+                at(OWNER, together, i - OWNER)
+                at(HAND, hand, i - HAND)
+                continue
+            for kind, f in enumerate((give, pair, together, hand)):
+                for e in range(done[kind], i - lags(j)[kind] + 1):
+                    f(e)
+                    done[kind] = e + 1
 
     def body(c, _):
         trip(c, False)
@@ -205,20 +250,33 @@
     trips = n_seq // SLOTS
     lax.fori_loop(0, trips - 1, body, 0)
     trip(trips - 1, True)
-    give(n_seq - 1)
-    for i in range(n_seq - PAIR, n_seq):
+    for i in range(done[1], n_seq):
         pair(i)
-    late = [(i + OWNER, together, i) for i in range(n_seq - OWNER, n_seq)] + [(i + HAND, hand, i) for i in range(n_seq - HAND, n_seq)]
-    for _, f, i in sorted(late, key=lambda x: x[0]):
-        f(i)
+    for i in range(done[2], owned):
+        together(i)
+    for i in range(owned, n_seq - 2):
+        everywhere(i)
+    for i in range(done[3], owned - 2):
+        hand(i)
+    for i in range(n_seq - 2, n_seq):
+        everywhere(i)
+    for i in range(owned - 2, owned):
+        hand(i)
 
     half = pl.ds(0, n_seq // 2)
     remote(mine.at[half], mine.at[half], pair_send, hand_recv, other).wait_send()
-    sent = pl.ds(0, n_seq // 2 - 2)
-    remote(part.at[sent], part.at[sent], part_send, hand_recv, other).wait_send()
-    remote(stat.at[sent], stat.at[sent], stat_send, hand_recv, other).wait_send()
-    sent = pl.ds(0, 2 * (chips - 1))
-    remote(out.at[sent], out.at[sent], out_send, hand_recv, other).wait_send()
+    fewer = functools.reduce(jnp.logical_or, [chip_of(i) == chip for i in range(owned, n_seq, 2)])
+    sent = pl.ds(0, owned // 2 - 2)
+    one = pl.ds(0, 1)
+    some = pl.ds(0, chips - 1)
+    for ref, sem in ((part, part_send), (stat, stat_send)):
+        remote(ref.at[sent], ref.at[sent], sem, hand_recv, other).wait_send()
+        pl.when(fewer)(remote(ref.at[one], ref.at[one], sem, hand_recv, other).wait_send)
+    for _ in range(LAST // 2):
+        remote(part.at[some], part.at[some], all_send.at[0], hand_recv, other).wait_send()
+        remote(stat.at[some], stat.at[some], all_send.at[1], hand_recv, other).wait_send()
+    remote(out.at[some], out.at[some], out_send, hand_recv, other).wait_send()
+    pl.when(jnp.logical_not(fewer))(remote(out.at[some], out.at[some], out_send, hand_recv, other).wait_send)
     handed = remote(out.at[half], out.at[half], hand_send, hand_recv, other)
     handed.wait_send()
     handed.wait_recv()
@@ -248,8 +306,10 @@
             pltpu.VMEM((n // 2, 2, heads), jnp.float32),
             pltpu.VMEM((2, chips, packed, 128), jnp.bfloat16),
             pltpu.VMEM((2, chips, 2, heads), jnp.float32),
-            dma(()), dma((SLOTS,)), dma((SLOTS,)), dma(()), dma((n // 2,)), dma(()), dma(()), dma((2,)), dma((2,)),
-            dma(()), dma((n // 2,)), dma(()), dma(()),
+            pltpu.VMEM((LAST // 2, chips, packed, 128), jnp.bfloat16),
+            pltpu.VMEM((LAST // 2, chips, 2, heads), jnp.float32),
+            dma((2,)), dma((SLOTS,)), dma((SLOTS,)), dma(()), dma((n // 2,)), dma(()), dma(()), dma((2,)), dma((2,)),
+            dma(()), dma((n // 2,)), dma(()), dma(()), dma((2,)), dma((LAST // 2, 2)),
         ],
         compiler_params=pltpu.CompilerParams(vmem_limit_bytes=60 * 1024 * 1024, collective_id=0, has_side_effects=True),
     )(q, kt, vt)

time: 41.7 us -> 40.2 us (0.964)
  Pallas kernels: 40.8 us -> 39.3 us
    pallas_call x1, Pallas kernels: 40.8 us -> 39.3 us  [attend(): pl.pallas_call(kernel, out_shape=pltpu.VMEM((n, heads, head), jnp.bfloat1...]
where the time goes in v3:
time: 40.2 us; the launch traced here: 40.1 us
  Pallas kernels  39.3 us (98%)
  local copies, waits for them, and re-layouts  0.8 us (2%)
    pallas_call x1, Pallas kernels, attend(): pl.pallas_call(kernel, out_shape=pltpu.VMEM((n, heads, head), jnp.bfloat1...  39.3 us

profile of v3, /device:TPU:0, one launch (start us, length us, event | category | flops | bytes accessed | tf_op | source)
XLA Modules:
  0.0 40.1 jit_solution(9413832076287667535)
XLA Ops:
  0.0 39.3 %shard_map.37 = bf16[32,32,160]{2,1,0:T(8,128)(2,1)S(1)} custom-call(bf16[32,32,160]{2,1,0:T(8,128)(2,1)} %q_hbm.1, bf16[32,1280,512]{2,1,0:T(8,128)(2,1)} %bitcast.6, bf16[32,1280,512]{2,1,0:T(8,128)(2,1)} %bitcast.7), custom_call_target="tpu_custom_call" | custom-call | tf_op jit(solution)/shard_map/pallas_call | solution.py:293
  39.3 0.8 %copy.5 = bf16[32,32,160]{2,1,0:T(8,128)(2,1)} copy(bf16[32,32,160]{2,1,0:T(8,128)(2,1)S(1)} %shard_map.37) | data formatting | bytes 655360

commit v4 on v3

--- a/solution.py
+++ b/solution.py
@@ -9,7 +9,7 @@
 MESH = pl.DeviceIdType.MESH
 AHEAD, LESS = 3, 3
 LATE = 2
-LAST = 4
+LAST = 2
 SLOTS = 8
 PAIR, OWNER, HAND = 3, 12, 20
 LOG2E = 1.4426950408889634
@@ -36,6 +36,7 @@
     chips = parts.shape[1]
     tail = head - 128
     owned = n_seq - LAST
+    peers = [2 * (d + (d + chips - chip) // chips) + core for d in range(chips - 1)]
 
     def remote(src, dst, send, recv, to):
         return pltpu.make_async_remote_copy(src, dst, send, recv, device_id={"sp": to}, device_id_type=MESH)
@@ -123,11 +124,9 @@
 
             if isinstance(i, int) and i >= owned:
                 slot = h - (n_seq - LAST) // 2
-                peers = [(me + 2 * d) % (2 * chips) for d in range(1, chips)]
+                stat[h] = jnp.where(lane == 0, high, total).T[:2, :heads]
                 for peer in peers:
                     remote(part.at[h], all_parts.at[slot, chip], all_send.at[0], all_recv.at[slot, 0], peer).start()
-                stat[h] = jnp.where(lane == 0, high, total).T[:2, :heads]
-                for peer in peers:
                     remote(stat.at[h], all_stats.at[slot, chip], all_send.at[1], all_recv.at[slot, 1], peer).start()
                 all_parts[slot, chip] = part[h]
                 all_stats[slot, chip] = stat[h]
@@ -175,8 +174,8 @@
         @pl.when(2 * chip_of(i) + i % 2 == me)
         def _():
             result(i, parts.at[rd], stats.at[rd], part_recv.at[rd], stat_recv.at[rd])
-            for d in range(1, chips):
-                remote(out.at[i], out.at[i], out_send, out_recv.at[i // 2], (me + 2 * d) % (2 * chips)).start()
+            for peer in peers:
+                remote(out.at[i], out.at[i], out_send, out_recv.at[i // 2], peer).start()
 
     def everywhere(i):
         slot = i // 2 - (n_seq - LAST) // 2
@@ -254,8 +253,6 @@
         pair(i)
     for i in range(done[2], owned):
         together(i)
-    for i in range(owned, n_seq - 2):
-        everywhere(i)
     for i in range(done[3], owned - 2):
         hand(i)
     for i in range(n_seq - 2, n_seq):

time: 40.2 us -> 39.7 us (0.988)
  Pallas kernels: 39.3 us -> 38.7 us
    pallas_call x1, Pallas kernels: 39.3 us -> 38.7 us  [attend(): pl.pallas_call(kernel, out_shape=pltpu.VMEM((n, heads, head), jnp.bfloat1...]
where the time goes in v4:
time: 39.7 us; the launch traced here: 39.5 us
  Pallas kernels  38.7 us (97%)
  local copies, waits for them, and re-layouts  0.8 us (2%)
    pallas_call x1, Pallas kernels, attend(): pl.pallas_call(kernel, out_shape=pltpu.VMEM((n, heads, head), jnp.bfloat1...  38.7 us
    unnamed x1, local copies, waits for them, and re-layouts  0.8 us

profile of v4, /device:TPU:0, one launch (start us, length us, event | category | flops | bytes accessed | tf_op | source)
XLA Modules:
  0.0 39.5 jit_solution(16062769694151074057)
XLA Ops:
  0.0 38.7 %shard_map.37 = bf16[32,32,160]{2,1,0:T(8,128)(2,1)S(1)} custom-call(bf16[32,32,160]{2,1,0:T(8,128)(2,1)} %q_hbm.1, bf16[32,1280,512]{2,1,0:T(8,128)(2,1)} %bitcast.6, bf16[32,1280,512]{2,1,0:T(8,128)(2,1)} %bitcast.7), custom_call_target="tpu_custom_call" | custom-call | tf_op jit(solution)/shard_map/pallas_call | solution.py:290
  38.7 0.8 %copy.5 = bf16[32,32,160]{2,1,0:T(8,128)(2,1)} copy(bf16[32,32,160]{2,1,0:T(8,128)(2,1)S(1)} %shard_map.37) | data formatting | bytes 655360
